TPU v7x, 32 devices: a whole 2x2x4 slice. The times are simulated.
32 devices in a mesh: pairs: 8 (over z, y), cols: 4 (over x, core).
Axes of the slice: x: 2, y: 2, z: 4, core: 2. Of those that a mesh axis runs over, the one named last changes fastest.
Arguments:
- amplitudes: bfloat16 [64, 256, 256], P('pairs', 'cols'), may hold values from -6 to 6
- pno_counts: int32 [64], P('pairs'), may hold values from 96 to 256
- fock_blocks: bfloat16 [64, 256, 256], P('pairs'), may hold values from -1 to 5, as said below
- exchange_blocks: bfloat16 [64, 256, 256], P('pairs', 'cols'), may hold values from -6 to 6
- intersections: bfloat16 [64, 32, 256, 256], P('pairs', None, 'cols'), may hold values from -0.375 to 0.375
- partners: int32 [64, 32], P('pairs'), may hold values from 0 to 63, as said below
- couplings: float32 [64, 32], P('pairs'), may hold values from -3 to 3
Outputs:
- residual_blocks: bfloat16 [64, 256, 256], P('pairs', 'cols')
Inputs may be any that keep to these rules, and one draw needn't show every extreme that they name: `partners`: within the coupling lists of one aligned block of 8 pairs, at most 64 entries name pairs of any one aligned block of 8 pairs, and exactly 64 do for some block. `fock_blocks`: each block is symmetric.
All inputs are finite; a program needn't handle non-finite values.
Results may differ from a plain program's by a relative error of at most 0.0022.
Values may be sent and summed in bfloat16 or wider, within the bound.
No kernel may reach another device: no remote copies, remote signals or barrier semaphores. Data moves between devices by JAX's collectives and lax.ppermute only.
A program may use at most 128 MiB of HBM per device.

v0:
```python
import jax
import jax.numpy as jnp
from jax import lax
from jax.sharding import PartitionSpec as P

CPL = 32


def shards(
    amplitudes, pno_counts, fock_blocks, exchange_blocks, intersections, partners, couplings
):
    local_pairs, share, width = amplitudes.shape
    column = lax.axis_index("cols")
    row_keep = column * share + jnp.arange(share, dtype=jnp.int32)[None, :] < pno_counts[:, None]
    col_keep = jnp.arange(width, dtype=jnp.int32)[None, :] < pno_counts[:, None]
    keep = row_keep[:, :, None] & col_keep[:, None, :]
    masked = jnp.where(keep, amplitudes, jnp.zeros_like(amplitudes))
    linear = partners.reshape(-1)
    empty = jnp.zeros((local_pairs * CPL, share, width), jnp.bfloat16)
    piece = lax.all_gather(masked, "pairs", axis=0, tiled=True)
    present = (linear >= 0) & (linear < piece.shape[0])
    picked = piece[jnp.clip(linear, 0, piece.shape[0] - 1)]
    partner_flat = jnp.where(present[:, None, None], picked, empty)
    partner_blocks = partner_flat.reshape(local_pairs, CPL, share, width)
    fock_cols = lax.dynamic_slice_in_dim(fock_blocks, column * share, share, 2)
    partial_value = jnp.einsum(
        "pab,pbc->pac", fock_cols, masked, preferred_element_type=jnp.float32
    )
    whole_intersections = lax.all_gather(intersections, "cols", axis=2, tiled=True)
    projected = jnp.einsum(
        "pqab,pqbc->pqac", partner_blocks, whole_intersections, preferred_element_type=jnp.float32
    ).astype(jnp.bfloat16)
    for slot_index in range(CPL):
        term = jnp.einsum(
            "pcd,pca->pda",
            intersections[:, slot_index],
            projected[:, slot_index],
            preferred_element_type=jnp.float32,
        )
        partial_value = partial_value + couplings[:, slot_index, None, None] * term
    summed = lax.psum_scatter(partial_value, "cols", scatter_dimension=1, tiled=True)
    fock_term = jnp.einsum("pab,pbc->pac", masked, fock_blocks, preferred_element_type=jnp.float32)
    total = exchange_blocks.astype(jnp.float32) + fock_term + summed
    return jnp.where(keep, total, jnp.zeros_like(total)).astype(jnp.bfloat16)


def solution(mesh):
    in_specs = (
        P("pairs", "cols", None),
        P("pairs"),
        P("pairs", None, None),
        P("pairs", "cols", None),
        P("pairs", None, "cols", None),
        P("pairs", None),
        P("pairs", None),
    )
    out_specs = P("pairs", "cols", None)
    return jax.shard_map(shards, mesh=mesh, in_specs=in_specs, out_specs=out_specs, check_vma=False)
```

profile of v0, /device:TPU:0, one launch (start us, length us, event | category | flops | bytes accessed | tf_op | source)
XLA Modules:
  0.0 406.6 jit_solution(1802354815083428256)
XLA Ops:
  8.1 1.8 and_select_fusion
  11.7 50.1 %all-gather.3.cloned.1.call-done = bf16[64,64,256]{2,1,0:T(8,128)(2,1)} async-done(((bf16[8,64,256]{2,1,0:T(8,128)(2,1)}), bf16[64,64,256]{2,1,0:T(8,128)(2,1)}) %all-gather.3.cloned.1.call-update) | async-done | bytes 2097168 | tf_op jit(solution)/shard_map/all_gather | solution.py:20
  61.9 12.4 %gather_fusion = bf16[256,64,256]{2,1,0:T(8,128)(2,1)} fusion(bf16[64,64,256]{2,1,0:T(8,128)(2,1)} %all-gather.3.cloned.1.call-done, s32[1024]{0:T(1024)S(1)} %pad_clamp_fusion), kind=kCustom, calls=%fused_computation | custom fusion | bytes 16778240 | tf_op jit(solution)/shard_map/gather | solution.py:22
  74.2 189.3 %all-gather.5.cloned.1.call-done = bf16[8,32,256,256]{3,2,1,0:T(8,128)(2,1)} async-done(((bf16[8,32,64,256]{3,2,1,0:T(8,128)(2,1)}), bf16[8,32,256,256]{3,2,1,0:T(8,128)(2,1)}) %all-gather.5.cloned.1.call-update) | async-done | bytes 33554448 | tf_op jit(solution)/shard_map/all_gather | solution.py:29
  263.5 15.6 %fusion.3 = bf16[8,32,64,256]{3,2,1,0:T(8,128)(2,1)S(1)} fusion(bf16[8,32,256,256]{3,2,1,0:T(8,128)(2,1)} %all-gather.5.cloned.1.call-done, bf16[8,32,64,256]{3,2,1,0:T(8,128)(2,1)} %bitcast.390, pred[8,32]{1,0:T(8,128)(4,1)S(1)} %compare_and_fusion), kind=kOutput, calls=%fused_computation.4 | convolution fusion | flops 2155872256 | bytes 50331904 | tf_op jit(solution)/shard_map/pqab,pqbc->pqac/dot_general | solution.py:30
  279.1 2.9 fusion.11
  282.0 2.8 fusion.12
  284.8 2.7 fusion.13
  287.6 2.9 fusion.14
  290.5 2.8 fusion.15
  293.3 2.8 fusion.16
  297.9 1.9 fusion.18
  299.7 1.8 fusion.19
  301.6 1.8 fusion.20
  305.2 1.8 fusion.22
  307.0 1.8 fusion.23
  308.8 1.9 fusion.24
  312.5 1.8 fusion.26
  314.3 1.8 fusion.27
  316.1 1.8 fusion.28
  317.9 1.9 fusion.29
  321.6 1.8 fusion.31
  323.4 1.8 fusion.32
  327.0 1.8 fusion.34
  328.8 1.8 fusion.35
  330.6 1.8 fusion.36
  332.4 1.9 fusion.37
  337.9 1.8 fusion.40
  341.5 1.8 fusion.42
  343.3 23.3 %bitcast_add_fusion = f32[8,256,256]{2,1,0:T(8,128)} fusion(f32[8,256,256]{1,2,0:T(8,128)} %fusion.11, f32[8,256,256]{1,2,0:T(8,128)} %fusion.12, f32[8,256,256]{1,2,0:T(8,128)} %fusion.13, f32[8,256,256]{1,2,0:T(8,128)} %fusion.14, f32[8,256,256]{1,2,0:T(8,128)} %fusion.15, f32[8,256,256]{1,2,0:T(8,128)} %fusion.16, f32[8,256,256]{1,2,0:T(8,128)} %fusion.17, ...), kind=kOutput, calls=%fused_computation.6 | convolution fusion | flops 100663296 | bytes 70008832 | tf_op jit(solution)/shard_map/pab,pbc->pac/dot_general | solution.py:26
  366.7 31.3 %reduce-scatter.2.cloned.1.call-done = f32[8,64,256]{2,1,0:T(8,128)} async-done(((f32[8,256,256]{2,1,0:T(8,128)}), f32[8,64,256]{2,1,0:T(8,128)}) %reduce-scatter.2.cloned.1.call-update) | async-done | bytes 524304 | tf_op jit(solution)/shard_map/reduce_scatter | solution.py:41
  398.0 2.1 fusion.9
  (39 shorter events, 17.6 us)
Async XLA Ops:
  6.5 336.8 %copy-start = (bf16[8,256,256]{2,1,0:T(8,128)(2,1)S(1)}, bf16[8,256,256]{2,1,0:T(8,128)(2,1)}, u32[]{:S(2)}) copy-start(bf16[8,256,256]{2,1,0:T(8,128)(2,1)} %param.9) | copy-start | bytes 3145732
  6.5 55.3 %all-gather.3.cloned.1.call-start = ((), (), s32[]{:S(2)}) async-start(), calls=%async_computation.1 | async-start | bytes 2359296 | tf_op jit(solution)/shard_map/all_gather | solution.py:20
  9.9 0.8 copy-start.4
  9.9 0.9 copy-start.2
  9.9 253.6 %all-gather.5.cloned.1.call-start = ((), (), s32[]{:S(2)}) async-start(), calls=%async_computation.2 | async-start | bytes 41943040 | tf_op jit(solution)/shard_map/all_gather | solution.py:29
  10.7 387.3 %reduce-scatter.2.cloned.1.call-start = ((), (), s32[]{:S(2)}) async-start(), calls=%async_computation.3 | async-start | bytes 2621440 | tf_op jit(solution)/shard_map/reduce_scatter | solution.py:41
  279.1 17.0 %slice-start = ((s8[8388608]{0:T(1024)(128)(4,1)}), s8[4194304]{0:T(1024)(128)(4,1)S(1)}, s32[]{:S(2)}) async-start(s8[8388608]{0:T(1024)(128)(4,1)} %bitcast.388), calls=%async_computation.4 | async-start | bytes 8388608
  287.6 8.5 %slice-start.1 = ((s8[8388608]{0:T(1024)(128)(4,1)}), s8[4194304]{0:T(1024)(128)(4,1)S(1)}, s32[]{:S(2)}) async-start(s8[8388608]{0:T(1024)(128)(4,1)} %bitcast.388), calls=%async_computation.5 | async-start | bytes 8388608
  339.7 3.6 copy-start.1
  366.6 31.3 %copy-start.3 = (bf16[8,64,256]{2,1,0:T(8,128)(2,1)S(1)}, bf16[8,64,256]{2,1,0:T(8,128)(2,1)}, u32[]{:S(2)}) copy-start(bf16[8,64,256]{2,1,0:T(8,128)(2,1)} %param.10) | copy-start | bytes 786436
Sparse Core Ops, SparseCore 0:
  10.0 51.7 all-gather.2
  63.4 200.0 all-gather.4
  366.8 31.1 reduce-scatter.1
where the time goes:
time: 407 us
  waiting for transfers between devices  271 us (67%)
  matrix products  105 us (26%)
  local copies, waits for them, and re-layouts  13.4 us (3%)
  between operations  13.2 us (3%)
    all_gather x1, waiting for transfers between devices, shards(): lax.all_gather(intersections, 'cols', axis=2, tiled=True)  189 us
    dot_general x32, matrix products, shards(): jnp.einsum('pcd,pca->pda', intersections[:, slot_index], projected[:, slo...  64.2 us
    all_gather x1, waiting for transfers between devices, shards(): piece = lax.all_gather(masked, 'pairs', axis=0, tiled=True)  50.1 us
    reduce_scatter x1, waiting for transfers between devices, shards(): lax.psum_scatter(partial_value, 'cols', scatter_dimension=1, tiled=True)  31.3 us
    dot_general x1, matrix products, shards(): jnp.einsum('pab,pbc->pac', fock_cols, masked, preferred_element_type=jnp....  23.3 us
    dot_general x1, matrix products, shards(): jnp.einsum('pqab,pqbc->pqac', partner_blocks, whole_intersections, prefer...  15.6 us
    gather x1, local copies, waits for them, and re-layouts, shards(): picked = piece[jnp.clip(linear, 0, piece.shape[0] - 1)]  12.4 us
  transfers between devices with their start and end apart: 3, of which 3 were waited for; matrix products, arithmetic and copies ran while one was open for 3% of the time, Pallas kernels for 0%

commit v1 on v0

--- a/solution.py
+++ b/solution.py
@@ -4,6 +4,24 @@
 from jax.sharding import PartitionSpec as P
 
 CPL = 32
+
+
+def cubes_create(panel, array_here):
+    big, step_out, after = (lax.axis_size("cols"), lax.axis_index("cols"), panel.shape[2])
+    sheets = [(dd, (dd + 1) % big) for dd in range(big)]
+    rows = [(dd, (dd - 1) % big) for dd in range(big)]
+    current_arr = big // 2
+    upper = a_now = panel
+    d_next = array_here(panel, step_out * after)
+    i0 = 1
+    while i0 < current_arr + 1:
+        upper = lax.ppermute(upper, "cols", sheets)
+        if i0 < big - current_arr:
+            a_now = lax.ppermute(a_now, "cols", rows)
+            d_next = d_next + array_here(a_now, (step_out + i0) % big * after)
+        d_next = d_next + array_here(upper, (step_out - i0) % big * after)
+        i0 += 1
+    return d_next
 
 
 def shards(
@@ -26,9 +44,14 @@
     partial_value = jnp.einsum(
         "pab,pbc->pac", fock_cols, masked, preferred_element_type=jnp.float32
     )
-    whole_intersections = lax.all_gather(intersections, "cols", axis=2, tiled=True)
-    projected = jnp.einsum(
-        "pqab,pqbc->pqac", partner_blocks, whole_intersections, preferred_element_type=jnp.float32
+    projected = cubes_create(
+        intersections,
+        lambda own_block, offset: jnp.einsum(
+            "pqab,pqbc->pqac",
+            lax.dynamic_slice_in_dim(partner_blocks, offset, own_block.shape[2], axis=3),
+            own_block,
+            preferred_element_type=jnp.float32,
+        ),
     ).astype(jnp.bfloat16)
     for slot_index in range(CPL):
         term = jnp.einsum(

time: 407 us -> 436 us (1.071)
  matrix products: 105 us -> 149 us
  waiting for transfers between devices: 271 us -> 243 us
  other arithmetic: 3.37 us -> 12 us
  starting transfers between devices: 0.08 us -> 4.97 us
    ppermute x0 -> x3, waiting for transfers between devices: none -> 208 us  [the longest x2 208 us: cubes_create(): upper = lax.ppermute(upper, 'cols', sheets)]
    all_gather x1 -> x0, waiting for transfers between devices: 189 us -> none  [shards(): lax.all_gather(intersections, 'cols', axis=2, tiled=True)]
    all_gather x1, waiting for transfers between devices: 50.1 us -> 0.01 us  [shards(): piece = lax.all_gather(masked, 'pairs', axis=0, tiled=True)]
    dot_general x1 -> x4, matrix products: 15.6 us -> 60.4 us  [shards(): jnp.einsum('pqab,pqbc->pqac', lax.dynamic_slice_in_dim(partner_blocks, of...]
    select_n x0 -> x1, other arithmetic: none -> 7.32 us  [shards(): partner_flat = jnp.where(present[:, None, None], picked, empty)]
    ppermute x0 -> x3, starting transfers between devices: none -> 4.93 us  [the longest x2 3.01 us: cubes_create(): upper = lax.ppermute(upper, 'cols', sheets)]
  transfers between devices with their start and end apart: 3 -> 5, of which waited for: 3 -> 3; matrix products, arithmetic and copies ran while one was open for 3% -> 14% of each run, Pallas kernels for 0% -> 0%
where the time goes in v1:
time: 436 us
  waiting for transfers between devices  243 us (56%)
  matrix products  149 us (34%)
  local copies, waits for them, and re-layouts  13.8 us (3%)
  between operations  13.5 us (3%)
  other arithmetic  12 us (3%)
  starting transfers between devices  4.97 us (1%)
    ppermute x2, waiting for transfers between devices, cubes_create(): upper = lax.ppermute(upper, 'cols', sheets)  208 us
    dot_general x32, matrix products, shards(): jnp.einsum('pcd,pca->pda', intersections[:, slot_index], projected[:, slo...  64.2 us
    dot_general x4, matrix products, shards(): jnp.einsum('pqab,pqbc->pqac', lax.dynamic_slice_in_dim(partner_blocks, of...  60.4 us
    reduce_scatter x1, waiting for transfers between devices, shards(): lax.psum_scatter(partial_value, 'cols', scatter_dimension=1, tiled=True)  35.2 us
    dot_general x1, matrix products, shards(): jnp.einsum('pab,pbc->pac', fock_cols, masked, preferred_element_type=jnp....  22.2 us
    gather x1, local copies, waits for them, and re-layouts, shards(): picked = piece[jnp.clip(linear, 0, piece.shape[0] - 1)]  10.2 us
  transfers between devices with their start and end apart: 5, of which 3 were waited for; matrix products, arithmetic and copies ran while one was open for 14% of the time, Pallas kernels for 0%

profile of v1, /device:TPU:0, one launch (start us, length us, event | category | flops | bytes accessed | tf_op | source)
XLA Modules:
  0.0 435.7 jit_solution(9594796857403258096)
XLA Ops:
  7.0 1.9 collective-permute-start
  12.3 175.4 %collective-permute-done.1 = bf16[8,32,64,256]{3,2,1,0:T(8,128)(2,1)} collective-permute-done((bf16[8,32,64,256]{3,2,1,0:T(8,128)(2,1)}, bf16[8,32,64,256]{3,2,1,0:T(8,128)(2,1)}, u32[]{:S(2)}, u32[]{:S(2)}) %collective-permute-start.1) | collective-permute-done | bytes 8388640 | tf_op jit(solution)/shard_map/ppermute | solution.py:18
  187.7 2.5 collective-permute-start.2
  192.5 1.9 slice_reduce_fusion.31
  195.2 10.2 %gather_fusion = bf16[256,64,256]{2,1,0:T(8,128)(2,1)} fusion(bf16[64,64,256]{2,1,0:T(8,128)(2,1)} %all-gather.2.cloned.1.call-done, s32[1024]{0:T(1024)S(1)} %pad_clamp_fusion), kind=kCustom, calls=%fused_computation | custom fusion | bytes 16778240 | tf_op jit(solution)/shard_map/gather | solution.py:40
  205.4 7.3 %broadcast_select_fusion = bf16[8,32,64,256]{3,2,1,0:T(8,128)(2,1)} fusion(bf16[8,32,64,256]{3,2,1,0:T(8,128)(2,1)} %bitcast.393, pred[8,32]{1,0:T(8,128)(4,1)S(1)} %compare_and_fusion), kind=kLoop, calls=%fused_computation.2 | loop fusion | flops 4194304 | bytes 16777472 | tf_op jit(solution)/shard_map/jit(_where)/select_n | solution.py:41
  212.7 12.9 %fusion.5 = f32[8,32,64,256]{3,2,1,0:T(8,128)} fusion(bf16[8,32,64,256]{3,2,1,0:T(8,128)(2,1)} %param.11, bf16[8,32,64,256]{3,2,1,0:T(8,128)(2,1)} %broadcast_select_fusion, s32[]{:T(128)S(6)} %select_n.52), kind=kOutput, calls=%fused_computation.8 | convolution fusion | flops 536870912 | bytes 29360132 | tf_op jit(solution)/shard_map/pqab,pqbc->pqac/dot_general | solution.py:49
  225.6 11.6 %fusion.1 = f32[8,32,64,256]{3,2,1,0:T(8,128)} fusion(bf16[8,32,64,256]{3,2,1,0:T(8,128)(2,1)} %collective-permute-done.1, bf16[8,32,64,256]{3,2,1,0:T(8,128)(2,1)S(1)} %copy-done.1, s32[]{:T(128)S(6)} %select_n.58), kind=kOutput, calls=%fused_computation.4 | convolution fusion | flops 536870912 | bytes 29360132 | tf_op jit(solution)/shard_map/pqab,pqbc->pqac/dot_general | solution.py:49
  237.2 11.5 %fusion.3 = f32[8,32,64,256]{3,2,1,0:T(8,128)} fusion(bf16[8,32,64,256]{3,2,1,0:T(8,128)(2,1)} %collective-permute-done, bf16[8,32,64,256]{3,2,1,0:T(8,128)(2,1)S(1)} %copy-done.1, s32[]{:T(128)S(6)} %select_n.56), kind=kOutput, calls=%fused_computation.6 | convolution fusion | flops 536870912 | bytes 29360132 | tf_op jit(solution)/shard_map/pqab,pqbc->pqac/dot_general | solution.py:49
  248.7 32.1 %collective-permute-done.2 = bf16[8,32,64,256]{3,2,1,0:T(8,128)(2,1)} collective-permute-done((bf16[8,32,64,256]{3,2,1,0:T(8,128)(2,1)}, bf16[8,32,64,256]{3,2,1,0:T(8,128)(2,1)}, u32[]{:S(2)}, u32[]{:S(2)}) %collective-permute-start.2) | collective-permute-done | bytes 8388640 | tf_op jit(solution)/shard_map/ppermute | solution.py:18
  280.9 24.3 %add_convert_fusion = bf16[8,32,64,256]{3,2,1,0:T(8,128)(2,1)} fusion(f32[8,32,64,256]{3,2,1,0:T(8,128)} %fusion.1, f32[8,32,64,256]{3,2,1,0:T(8,128)} %fusion.5, f32[8,32,64,256]{3,2,1,0:T(8,128)} %fusion.3, bf16[8,32,64,256]{3,2,1,0:T(8,128)(2,1)} %collective-permute-done.2, bf16[8,32,64,256]{3,2,1,0:T(8,128)(2,1)} %broadcast_select_fusion, s32[]{:T(128)S(6)} %select_n.60), kind=kOutput, calls=%fused_computation.1 | convolution fusion | flops 553648128 | bytes 71303168 | tf_op jit(solution)/shard_map/pqab,pqbc->pqac/dot_general | solution.py:49
  308.4 2.8 fusion.13
  311.2 3.0 fusion.14
  314.2 3.0 fusion.15
  317.2 3.2 fusion.16
  320.4 2.8 fusion.17
  323.2 2.8 fusion.18
  326.0 1.8 fusion.19
  327.8 1.8 fusion.20
  329.6 1.8 fusion.21
  335.1 1.8 fusion.24
  336.9 1.9 fusion.25
  340.5 1.8 fusion.27
  342.4 1.8 fusion.28
  346.0 1.8 fusion.30
  351.4 1.8 fusion.33
  355.0 1.8 fusion.35
  360.4 1.8 fusion.38
  365.8 1.8 fusion.41
  369.4 22.2 %bitcast_add_fusion = f32[8,256,256]{2,1,0:T(8,128)} fusion(f32[8,256,256]{1,2,0:T(8,128)S(1)} %fusion.11, f32[8,256,256]{1,2,0:T(8,128)S(1)} %fusion.12, f32[8,256,256]{1,2,0:T(8,128)} %fusion.13, f32[8,256,256]{1,2,0:T(8,128)} %fusion.14, f32[8,256,256]{1,2,0:T(8,128)} %fusion.15, f32[8,256,256]{1,2,0:T(8,128)} %fusion.16, f32[8,256,256]{1,2,0:T(8,128)} %fusion.17, ...), kind=kOutput, calls=%fused_computation.10 | convolution fusion | flops 100663296 | bytes 70008832 | tf_op jit(solution)/shard_map/pab,pbc->pac/dot_general | solution.py:44
  391.6 35.2 %reduce-scatter.2.cloned.1.call-done = f32[8,64,256]{2,1,0:T(8,128)} async-done(((f32[8,256,256]{2,1,0:T(8,128)}), f32[8,64,256]{2,1,0:T(8,128)}) %reduce-scatter.2.cloned.1.call-update) | async-done | bytes 524304 | tf_op jit(solution)/shard_map/reduce_scatter | solution.py:64
  426.8 2.1 fusion.9
  (46 shorter events, 31.5 us)
Async XLA Ops:
  6.5 362.9 %copy-start = (bf16[8,256,256]{2,1,0:T(8,128)(2,1)S(1)}, bf16[8,256,256]{2,1,0:T(8,128)(2,1)}, u32[]{:S(2)}) copy-start(bf16[8,256,256]{2,1,0:T(8,128)(2,1)} %param.9) | copy-start | bytes 3145732
  6.5 188.6 %all-gather.2.cloned.1.call-start = ((), (), s32[]{:S(2)}) async-start(), calls=%async_computation.1 | async-start | bytes 2359296 | tf_op jit(solution)/shard_map/all_gather | solution.py:38
  6.5 181.1 %collective-permute-start.1 = (bf16[8,32,64,256]{3,2,1,0:T(8,128)(2,1)}, bf16[8,32,64,256]{3,2,1,0:T(8,128)(2,1)}, u32[]{:S(2)}, u32[]{:S(2)}) collective-permute-start(bf16[8,32,64,256]{3,2,1,0:T(8,128)(2,1)} %param.11), channel_id=1, source_target_pairs={{0,1},{1,2},{2,3},{3,0},{4,5},{5,6},{6,7},{7,4},{8,9},{9,10},{10,1... | collective-permute-start | bytes 25165832 | tf_op jit(solution)/shard_map/ppermute | solution.py:18
  7.0 230.2 %collective-permute-start = (bf16[8,32,64,256]{3,2,1,0:T(8,128)(2,1)}, bf16[8,32,64,256]{3,2,1,0:T(8,128)(2,1)}, u32[]{:S(2)}, u32[]{:S(2)}) collective-permute-start(bf16[8,32,64,256]{3,2,1,0:T(8,128)(2,1)} %param.11), channel_id=1, source_target_pairs={{0,3},{1,0},{2,1},{3,2},{4,7},{5,4},{6,5},{7,6},{8,11},{9,8},{10,9... | collective-permute-start | bytes 25165832 | tf_op jit(solution)/shard_map/ppermute | solution.py:20
  12.2 414.6 %reduce-scatter.2.cloned.1.call-start = ((), (), s32[]{:S(2)}) async-start(), calls=%async_computation.2 | async-start | bytes 2621440 | tf_op jit(solution)/shard_map/reduce_scatter | solution.py:64
  187.7 93.2 %collective-permute-start.2 = (bf16[8,32,64,256]{3,2,1,0:T(8,128)(2,1)}, bf16[8,32,64,256]{3,2,1,0:T(8,128)(2,1)}, u32[]{:S(2)}, u32[]{:S(2)}) collective-permute-start(bf16[8,32,64,256]{3,2,1,0:T(8,128)(2,1)} %collective-permute-done.1), channel_id=1, source_target_pairs={{0,1},{1,2},{2,3},{3,0},{4,5},{5,6},{6,7},{7,4},{8,9},{9,10},{10,1... | collective-permute-start | bytes 25165832 | tf_op jit(solution)/shard_map/ppermute | solution.py:18
  212.7 12.9 %copy-start.1 = (bf16[8,32,64,256]{3,2,1,0:T(8,128)(2,1)S(1)}, bf16[8,32,64,256]{3,2,1,0:T(8,128)(2,1)}, u32[]{:S(2)}) copy-start(bf16[8,32,64,256]{3,2,1,0:T(8,128)(2,1)} %broadcast_select_fusion) | copy-start | bytes 25165828
  305.2 15.2 %slice-start = ((s8[8388608]{0:T(1024)(128)(4,1)}), s8[4194304]{0:T(1024)(128)(4,1)S(1)}, s32[]{:S(2)}) async-start(s8[8388608]{0:T(1024)(128)(4,1)} %bitcast.391), calls=%async_computation.3 | async-start | bytes 8388608
  311.2 9.2 %slice-start.1 = ((s8[8388608]{0:T(1024)(128)(4,1)}), s8[4194304]{0:T(1024)(128)(4,1)S(1)}, s32[]{:S(2)}) async-start(s8[8388608]{0:T(1024)(128)(4,1)} %bitcast.391), calls=%async_computation.4 | async-start | bytes 8388608
  314.2 11.8 %copy-start.2 = (bf16[8,32,64,256]{3,2,1,0:T(8,128)(2,1)S(1)}, bf16[8,32,64,256]{3,2,1,0:T(8,128)(2,1)}, u32[]{:S(2)}) copy-start(bf16[8,32,64,256]{3,2,1,0:T(8,128)(2,1)} %add_convert_fusion) | copy-start | bytes 25165828
  365.8 3.6 copy-start.3
  391.6 35.2 %copy-start.4 = (bf16[8,64,256]{2,1,0:T(8,128)(2,1)S(1)}, bf16[8,64,256]{2,1,0:T(8,128)(2,1)}, u32[]{:S(2)}) copy-start(bf16[8,64,256]{2,1,0:T(8,128)(2,1)} %param.10) | copy-start | bytes 786436
Sparse Core Ops, SparseCore 0:
  12.4 51.1 all-gather.1
  391.7 35.0 reduce-scatter.1
